TPU v7x, 32 devices: a whole 2x2x4 slice. The times are simulated.
32 devices in a mesh: dp: 8 (over y, x, core), expert: 4 (over z).
Axes of the slice: x: 2, y: 2, z: 4, core: 2. Of those that a mesh axis runs over, the one named last changes fastest.
Arguments:
- grad_out: bfloat16 [4, 2048, 1024], P(None, ('dp', 'expert')), may hold values from -12 to 12
- routes: int32 [4, 2048, 8], P(None, ('dp', 'expert')), may hold values from 0 to 127, all different within a row; in each aligned block of 64 rows (0 to 63, 64 to 127, ..., all dimensions but the last counted through in order) at most 8 rows name the same one
- route_probs: bfloat16 [4, 2048, 8], P(None, ('dp', 'expert')), may hold values from 0.049804688 to 0.3984375
- dispatched: bfloat16 [4, 1024, 1024], P(None, ('dp', 'expert')), may hold values from -12 to 12, as said below
- w_gate: bfloat16 [1024, 1024], P(None, 'expert'), may hold values from -0.1875 to 0.1875
- w_up: bfloat16 [1024, 1024], P(None, 'expert'), may hold values from -0.1875 to 0.1875
- w_down: bfloat16 [1024, 1024], P('expert'), may hold values from -0.25 to 0.25
Outputs:
- grad_in: bfloat16 [4, 2048, 1024], P(None, ('dp', 'expert'))
- grad_gate: float32 [1024, 1024], P('dp', 'expert')
- grad_up: float32 [1024, 1024], P('dp', 'expert')
- grad_down_t: float32 [1024, 1024], P('dp', 'expert')
Inputs may be any that keep to these rules, and one draw needn't show every extreme that they name: `routes`: in each micro-batch, among the 64 rows of one device no expert is named more than 8 times, a bound that some expert reaches in some of these blocks. `dispatched`: within each group of 4 consecutive blocks of 32 rows, blocks 2e and 2e + 1 are equal.
All inputs are finite; a program needn't handle non-finite values.
Results may differ from a plain program's by a relative error of at most 0.0058.
Values may be sent and summed in bfloat16 or wider, within the bound.
A program may use at most 64 MiB of HBM per device.

v0:
```python
import jax
import jax.numpy as jnp
from jax import lax
from jax.sharding import PartitionSpec as P

TOPK = 8
CAPS = 8


def swapped(x, axis, stride):
    return lax.ppermute(x, axis, [(i, i ^ 1 << stride) for i in range(lax.axis_size(axis))])


def slot_take(route_ids, targets, flat_dy, flat_probs, capacity):
    hitting = (route_ids == targets[:, None]).astype(jnp.int32)
    ranking = jnp.cumsum(hitting, axis=1) - 1
    chosen = hitting[:, None, :] * (
        ranking[:, None, :] == jnp.arange(capacity, dtype=jnp.int32)[None, :, None]
    ).astype(jnp.int32)
    position = jnp.sum(
        chosen * jnp.arange(route_ids.shape[1], dtype=jnp.int32)[None, None, :], axis=2
    )
    living = jnp.sum(chosen, axis=2) > 0
    weights = jnp.take_along_axis(flat_probs, position, axis=1)
    rows_at = position // TOPK
    picked = jnp.take(flat_dy, rows_at.reshape(-1), axis=0)
    scaled = (weights.reshape(-1, 1).astype(jnp.float32) * picked.astype(jnp.float32)).astype(
        jnp.bfloat16
    )
    return jnp.where(living.reshape(-1, 1), scaled, jnp.zeros_like(scaled))


def contract_rows(left, right):
    return lax.dot_general(
        left, right, (((0,), (0,)), ((), ())), preferred_element_type=jnp.float32
    )


def contract_cols(left, right):
    return lax.dot_general(
        left, right, (((1,), (1,)), ((), ())), preferred_element_type=jnp.float32
    )


def per_device(grad_out, routes, route_probs, dispatched, w_gate, w_up, w_down):
    groups = lax.axis_size("expert")
    member = lax.axis_index("expert")
    window = groups // 2
    tok_dev = grad_out.shape[1]
    model_width = grad_out.shape[2]
    half_cols = w_gate.shape[1]
    capacity = CAPS
    half_caps = capacity // 2
    slot_count = groups * capacity
    parity = member % 2
    acc_gate = jnp.zeros((model_width, half_cols), jnp.float32)
    acc_up = jnp.zeros((model_width, half_cols), jnp.float32)
    acc_down = jnp.zeros((model_width, half_cols), jnp.float32)
    outputs = []
    for micro_idx in range(grad_out.shape[0]):
        own_ids = routes[micro_idx]
        targets = jnp.arange(window, dtype=jnp.int32)
        flat_ids = jnp.broadcast_to(own_ids.reshape(1, -1), (window, tok_dev * TOPK))
        flat_probs = jnp.broadcast_to(
            route_probs[micro_idx].reshape(1, -1), (window, tok_dev * TOPK)
        )
        sending = slot_take(flat_ids, targets, grad_out[micro_idx], flat_probs, capacity)
        arrived = lax.all_to_all(
            sending.reshape(groups, half_caps, model_width),
            "expert",
            split_axis=0,
            concat_axis=0,
            tiled=True,
        )
        partner_rows = swapped(arrived, "expert", 0)
        lower = jnp.where(parity == 0, arrived, partner_rows)
        upper = jnp.where(parity == 0, partner_rows, arrived)
        scaled = jnp.concatenate([lower, upper], axis=1).reshape(slot_count, model_width)
        inputs = dispatched[micro_idx]
        gate_pre = jnp.dot(inputs, w_gate, preferred_element_type=jnp.float32)
        up_pre = jnp.dot(inputs, w_up, preferred_element_type=jnp.float32)
        sigmoid = jax.nn.sigmoid(gate_pre)
        activated = gate_pre * sigmoid
        hidden = (activated * up_pre).astype(jnp.bfloat16)
        acc_down = acc_down + contract_rows(scaled, hidden)
        dhidden = contract_cols(scaled, w_down)
        d_gate = (dhidden * up_pre * sigmoid * (1.0 + gate_pre * (1.0 - sigmoid))).astype(
            jnp.bfloat16
        )
        d_up = (dhidden * activated).astype(jnp.bfloat16)
        acc_gate = acc_gate + contract_rows(inputs, d_gate)
        acc_up = acc_up + contract_rows(inputs, d_up)
        partial_value = contract_cols(d_gate, w_gate) + contract_cols(d_up, w_up)
        returned = lax.all_to_all(
            partial_value.reshape(groups, capacity, model_width),
            "expert",
            split_axis=0,
            concat_axis=0,
            tiled=True,
        )
        summed = jnp.sum(returned.reshape(window, 2, capacity, model_width), axis=1)
        inside = own_ids < window
        hitting = (
            own_ids.reshape(-1)[:, None] == jnp.arange(window, dtype=jnp.int32)[None, :]
        ).astype(jnp.int32)
        ranking = jnp.sum((jnp.cumsum(hitting, axis=0) - 1) * hitting, axis=1).reshape(
            tok_dev, TOPK
        )
        slot_keys = jnp.where(inside, own_ids * capacity + ranking, -1)
        mixing = jnp.sum(
            (
                slot_keys[:, :, None]
                == jnp.arange(window * capacity, dtype=jnp.int32)[None, None, :]
            ).astype(jnp.float32),
            axis=1,
        )
        grad_tokens = jnp.dot(
            mixing,
            summed.reshape(window * capacity, model_width),
            precision=lax.Precision.HIGHEST,
            preferred_element_type=jnp.float32,
        )
        outputs.append(grad_tokens.astype(jnp.bfloat16))
    reduced = (
        lax.psum_scatter(acc_gate, "dp", scatter_dimension=0, tiled=True),
        lax.psum_scatter(acc_up, "dp", scatter_dimension=0, tiled=True),
        lax.psum_scatter(acc_down, "dp", scatter_dimension=0, tiled=True),
    )
    factor = 1.0 / (grad_out.shape[0] * lax.axis_size("dp"))
    return (jnp.stack(outputs), reduced[0] * factor, reduced[1] * factor, reduced[2] * factor)


def solution(mesh):
    return jax.shard_map(
        per_device,
        mesh=mesh,
        in_specs=(
            P(None, ("dp", "expert"), None),
            P(None, ("dp", "expert"), None),
            P(None, ("dp", "expert"), None),
            P(None, ("dp", "expert"), None),
            P(None, "expert"),
            P(None, "expert"),
            P("expert", None),
        ),
        out_specs=(
            P(None, ("dp", "expert"), None),
            P("dp", "expert"),
            P("dp", "expert"),
            P("dp", "expert"),
        ),
        check_vma=False,
    )
```

profile of v0, /device:TPU:0, one launch (start us, length us, event | category | flops | bytes accessed | tf_op | source)
XLA Modules:
  0.0 188.9 jit_solution(18175083567258758894)
XLA Ops:
  7.2 0.8 fusion.105
  13.1 6.3 %all-to-all-start.2 = ((bf16[4,4,1024]{2,1,0:T(4,128)(2,1)}), bf16[4,4,1024]{2,1,0:T(4,128)(2,1)S(1)}, u32[]{:S(2)}, u32[]{:S(2)}) async-start(bf16[4,4,1024]{2,1,0:T(4,128)(2,1)} %reshape.522), calls=%async_computation.2 | async-start | bytes 65536 | tf_op jit(solution)/shard_map/all_to_all | solution.py:68
  33.8 5.1 %all-to-all-start = ((bf16[4,4,1024]{2,1,0:T(4,128)(2,1)}), bf16[4,4,1024]{2,1,0:T(4,128)(2,1)S(1)}, u32[]{:S(2)}, u32[]{:S(2)}) async-start(bf16[4,4,1024]{2,1,0:T(4,128)(2,1)} %reshape.515), calls=%async_computation | async-start | bytes 65536 | tf_op jit(solution)/shard_map/all_to_all | solution.py:68
  39.7 4.9 %all-to-all-done = bf16[4,4,1024]{2,1,0:T(4,128)(2,1)S(1)} async-done(((bf16[4,4,1024]{2,1,0:T(4,128)(2,1)}), bf16[4,4,1024]{2,1,0:T(4,128)(2,1)S(1)}, u32[]{:S(2)}, u32[]{:S(2)}) %all-to-all-start) | async-done | bytes 32800 | tf_op jit(solution)/shard_map/all_to_all | solution.py:68
  44.6 3.3 %all-to-all-start.4 = ((bf16[4,4,1024]{2,1,0:T(4,128)(2,1)}), bf16[4,4,1024]{2,1,0:T(4,128)(2,1)S(1)}, u32[]{:S(2)}, u32[]{:S(2)}) async-start(bf16[4,4,1024]{2,1,0:T(4,128)(2,1)} %reshape.529), calls=%async_computation.4 | async-start | bytes 65536 | tf_op jit(solution)/shard_map/all_to_all | solution.py:68
  48.6 2.0 %collective-permute-start.1 = (bf16[4,4,1024]{2,1,0:T(4,128)(2,1)S(1)}, bf16[4,4,1024]{2,1,0:T(4,128)(2,1)S(1)}, u32[]{:S(2)}, u32[]{:S(2)}) collective-permute-start(bf16[4,4,1024]{2,1,0:T(4,128)(2,1)S(1)} %all-to-all-done.2), channel_id=1, source_target_pairs={{0,1},{1,0},{2,3},{3,2},{4,5},{5,4},{6,7},{7,6},{8,9},{9,8},{10,11... | collective-permute-start | bytes 98312 | tf_op jit(solution)/shard_map/ppermute | solution.py:11
  50.6 2.9 %all-to-all-done.4 = bf16[4,4,1024]{2,1,0:T(4,128)(2,1)S(1)} async-done(((bf16[4,4,1024]{2,1,0:T(4,128)(2,1)}), bf16[4,4,1024]{2,1,0:T(4,128)(2,1)S(1)}, u32[]{:S(2)}, u32[]{:S(2)}) %all-to-all-start.4) | async-done | bytes 32800 | tf_op jit(solution)/shard_map/all_to_all | solution.py:68
  53.5 3.3 %all-to-all-start.6 = ((bf16[4,4,1024]{2,1,0:T(4,128)(2,1)}), bf16[4,4,1024]{2,1,0:T(4,128)(2,1)S(1)}, u32[]{:S(2)}, u32[]{:S(2)}) async-start(bf16[4,4,1024]{2,1,0:T(4,128)(2,1)} %reshape.536), calls=%async_computation.6 | async-start | bytes 65536 | tf_op jit(solution)/shard_map/all_to_all | solution.py:68
  56.9 2.0 %collective-permute-start = (bf16[4,4,1024]{2,1,0:T(4,128)(2,1)S(1)}, bf16[4,4,1024]{2,1,0:T(4,128)(2,1)S(1)}, u32[]{:S(2)}, u32[]{:S(2)}) collective-permute-start(bf16[4,4,1024]{2,1,0:T(4,128)(2,1)S(1)} %all-to-all-done), channel_id=1, source_target_pairs={{0,1},{1,0},{2,3},{3,2},{4,5},{5,4},{6,7},{7,6},{8,9},{9,8},{10,11... | collective-permute-start | bytes 98312 | tf_op jit(solution)/shard_map/ppermute | solution.py:11
  58.9 3.4 %all-to-all-done.6 = bf16[4,4,1024]{2,1,0:T(4,128)(2,1)S(1)} async-done(((bf16[4,4,1024]{2,1,0:T(4,128)(2,1)}), bf16[4,4,1024]{2,1,0:T(4,128)(2,1)S(1)}, u32[]{:S(2)}, u32[]{:S(2)}) %all-to-all-start.6) | async-done | bytes 32800 | tf_op jit(solution)/shard_map/all_to_all | solution.py:68
  66.3 1.3 convolution_add_fusion
  67.9 0.9 fusion.5
  68.9 3.3 %all-to-all-start.1 = ((f32[4,8,1024]{2,1,0:T(8,128)}), f32[4,8,1024]{2,1,0:T(8,128)S(1)}, u32[]{:S(2)}, u32[]{:S(2)}) async-start(f32[4,8,1024]{2,1,0:T(8,128)} %fusion.5), calls=%async_computation.1 | async-start | bytes 262144 | tf_op jit(solution)/shard_map/all_to_all | solution.py:94
  73.8 1.4 fusion
  75.2 0.9 fusion.4
  76.4 0.9 fusion.3
  78.3 1.3 fusion.1
  79.9 5.0 %all-to-all-start.3 = ((f32[4,8,1024]{2,1,0:T(8,128)}), f32[4,8,1024]{2,1,0:T(8,128)S(1)}, u32[]{:S(2)}, u32[]{:S(2)}) async-start(f32[4,8,1024]{2,1,0:T(8,128)} %fusion.4), calls=%async_computation.3 | async-start | bytes 262144 | tf_op jit(solution)/shard_map/all_to_all | solution.py:94
  84.9 0.9 fusion.2
  85.8 5.0 %all-to-all-done.3 = f32[4,8,1024]{2,1,0:T(8,128)S(1)} async-done(((f32[4,8,1024]{2,1,0:T(8,128)}), f32[4,8,1024]{2,1,0:T(8,128)S(1)}, u32[]{:S(2)}, u32[]{:S(2)}) %all-to-all-start.3) | async-done | bytes 131104 | tf_op jit(solution)/shard_map/all_to_all | solution.py:94
  90.8 3.3 %all-to-all-start.5 = ((f32[4,8,1024]{2,1,0:T(8,128)}), f32[4,8,1024]{2,1,0:T(8,128)S(1)}, u32[]{:S(2)}, u32[]{:S(2)}) async-start(f32[4,8,1024]{2,1,0:T(8,128)} %fusion.3), calls=%async_computation.5 | async-start | bytes 262144 | tf_op jit(solution)/shard_map/all_to_all | solution.py:94
  94.6 5.6 %all-to-all-done.5 = f32[4,8,1024]{2,1,0:T(8,128)S(1)} async-done(((f32[4,8,1024]{2,1,0:T(8,128)}), f32[4,8,1024]{2,1,0:T(8,128)S(1)}, u32[]{:S(2)}, u32[]{:S(2)}) %all-to-all-start.5) | async-done | bytes 131104 | tf_op jit(solution)/shard_map/all_to_all | solution.py:94
  100.1 3.9 %all-to-all-start.7 = ((f32[4,8,1024]{2,1,0:T(8,128)}), f32[4,8,1024]{2,1,0:T(8,128)S(1)}, u32[]{:S(2)}, u32[]{:S(2)}) async-start(f32[4,8,1024]{2,1,0:T(8,128)} %fusion.2), calls=%async_computation.7 | async-start | bytes 262144 | tf_op jit(solution)/shard_map/all_to_all | solution.py:94
  104.8 5.1 %all-to-all-done.7 = f32[4,8,1024]{2,1,0:T(8,128)S(1)} async-done(((f32[4,8,1024]{2,1,0:T(8,128)}), f32[4,8,1024]{2,1,0:T(8,128)S(1)}, u32[]{:S(2)}, u32[]{:S(2)}) %all-to-all-start.7) | async-done | bytes 131104 | tf_op jit(solution)/shard_map/all_to_all | solution.py:94
  110.3 0.9 pad_maximum_fusion
  111.2 0.9 broadcast_multiply_fusion
  112.1 0.8 copy.55
  112.8 28.7 %reduce-scatter.6.cloned.1.call-done = f32[128,256]{0,1:T(8,128)} async-done(((f32[1024,256]{0,1:T(8,128)}), f32[128,256]{0,1:T(8,128)}) %reduce-scatter.6.cloned.1.call-update) | async-done | bytes 131088 | tf_op jit(solution)/shard_map/reduce_scatter | solution.py:126
  141.6 0.9 broadcast_multiply_fusion.1
  143.2 37.5 %reduce-scatter.4.cloned.1.call-done = f32[128,256]{0,1:T(8,128)} async-done(((f32[1024,256]{0,1:T(8,128)}), f32[128,256]{0,1:T(8,128)}) %reduce-scatter.4.cloned.1.call-update) | async-done | bytes 131088 | tf_op jit(solution)/shard_map/reduce_scatter | solution.py:125
  180.7 0.9 broadcast_multiply_fusion.2
  181.7 0.8 copy.53
  (197 shorter events, 30.2 us)
Async XLA Ops:
  7.2 13.9 %copy-start = (bf16[1024,256]{1,0:T(8,128)(2,1)S(1)}, bf16[1024,256]{1,0:T(8,128)(2,1)}, u32[]{:S(2)}) copy-start(bf16[1024,256]{1,0:T(8,128)(2,1)} %param.15) | copy-start | bytes 1572868
  7.2 4.4 %copy-start.4 = (bf16[4,64,1024]{2,1,0:T(8,128)(2,1)S(1)}, bf16[4,64,1024]{2,1,0:T(8,128)(2,1)}, u32[]{:S(2)}) copy-start(bf16[4,64,1024]{2,1,0:T(8,128)(2,1)} %param.11) | copy-start | bytes 1572868
  11.7 9.3 %copy-start.3 = (bf16[4,32,1024]{2,1,0:T(8,128)(2,1)S(1)}, bf16[4,32,1024]{2,1,0:T(8,128)(2,1)}, u32[]{:S(2)}) copy-start(bf16[4,32,1024]{2,1,0:T(8,128)(2,1)} %param.14) | copy-start | bytes 786436
  13.1 20.8 %all-to-all-start.2 = ((bf16[4,4,1024]{2,1,0:T(4,128)(2,1)}), bf16[4,4,1024]{2,1,0:T(4,128)(2,1)S(1)}, u32[]{:S(2)}, u32[]{:S(2)}) async-start(bf16[4,4,1024]{2,1,0:T(4,128)(2,1)} %reshape.522), calls=%async_computation.2 | async-start | bytes 65536 | tf_op jit(solution)/shard_map/all_to_all | solution.py:68
  21.1 1.0 copy-start.1
  33.8 10.8 %all-to-all-start = ((bf16[4,4,1024]{2,1,0:T(4,128)(2,1)}), bf16[4,4,1024]{2,1,0:T(4,128)(2,1)S(1)}, u32[]{:S(2)}, u32[]{:S(2)}) async-start(bf16[4,4,1024]{2,1,0:T(4,128)(2,1)} %reshape.515), calls=%async_computation | async-start | bytes 65536 | tf_op jit(solution)/shard_map/all_to_all | solution.py:68
  44.6 8.9 %all-to-all-start.4 = ((bf16[4,4,1024]{2,1,0:T(4,128)(2,1)}), bf16[4,4,1024]{2,1,0:T(4,128)(2,1)S(1)}, u32[]{:S(2)}, u32[]{:S(2)}) async-start(bf16[4,4,1024]{2,1,0:T(4,128)(2,1)} %reshape.529), calls=%async_computation.4 | async-start | bytes 65536 | tf_op jit(solution)/shard_map/all_to_all | solution.py:68
  48.6 14.5 %collective-permute-start.1 = (bf16[4,4,1024]{2,1,0:T(4,128)(2,1)S(1)}, bf16[4,4,1024]{2,1,0:T(4,128)(2,1)S(1)}, u32[]{:S(2)}, u32[]{:S(2)}) collective-permute-start(bf16[4,4,1024]{2,1,0:T(4,128)(2,1)S(1)} %all-to-all-done.2), channel_id=1, source_target_pairs={{0,1},{1,0},{2,3},{3,2},{4,5},{5,4},{6,7},{7,6},{8,9},{9,8},{10,11... | collective-permute-start | bytes 98312 | tf_op jit(solution)/shard_map/ppermute | solution.py:11
  53.5 8.9 %all-to-all-start.6 = ((bf16[4,4,1024]{2,1,0:T(4,128)(2,1)}), bf16[4,4,1024]{2,1,0:T(4,128)(2,1)S(1)}, u32[]{:S(2)}, u32[]{:S(2)}) async-start(bf16[4,4,1024]{2,1,0:T(4,128)(2,1)} %reshape.536), calls=%async_computation.6 | async-start | bytes 65536 | tf_op jit(solution)/shard_map/all_to_all | solution.py:68
  56.8 54.4 %reduce-scatter.8.cloned.1.call-start = ((), (), s32[]{:S(2)}) async-start(), calls=%async_computation.13 | async-start | bytes 1179648 | tf_op jit(solution)/shard_map/reduce_scatter | solution.py:127
  56.9 6.3 %collective-permute-start = (bf16[4,4,1024]{2,1,0:T(4,128)(2,1)S(1)}, bf16[4,4,1024]{2,1,0:T(4,128)(2,1)S(1)}, u32[]{:S(2)}, u32[]{:S(2)}) collective-permute-start(bf16[4,4,1024]{2,1,0:T(4,128)(2,1)S(1)} %all-to-all-done), channel_id=1, source_target_pairs={{0,1},{1,0},{2,3},{3,2},{4,5},{5,4},{6,7},{7,6},{8,9},{9,8},{10,11... | collective-permute-start | bytes 98312 | tf_op jit(solution)/shard_map/ppermute | solution.py:11
  58.9 6.3 %collective-permute-start.2 = (bf16[4,4,1024]{2,1,0:T(4,128)(2,1)S(1)}, bf16[4,4,1024]{2,1,0:T(4,128)(2,1)S(1)}, u32[]{:S(2)}, u32[]{:S(2)}) collective-permute-start(bf16[4,4,1024]{2,1,0:T(4,128)(2,1)S(1)} %all-to-all-done.4), channel_id=1, source_target_pairs={{0,1},{1,0},{2,3},{3,2},{4,5},{5,4},{6,7},{7,6},{8,9},{9,8},{10,11... | collective-permute-start | bytes 98312 | tf_op jit(solution)/shard_map/ppermute | solution.py:11
  62.4 3.9 %collective-permute-start.3 = (bf16[4,4,1024]{2,1,0:T(4,128)(2,1)S(1)}, bf16[4,4,1024]{2,1,0:T(4,128)(2,1)S(1)}, u32[]{:S(2)}, u32[]{:S(2)}) collective-permute-start(bf16[4,4,1024]{2,1,0:T(4,128)(2,1)S(1)} %all-to-all-done.6), channel_id=1, source_target_pairs={{0,1},{1,0},{2,3},{3,2},{4,5},{5,4},{6,7},{7,6},{8,9},{9,8},{10,11... | collective-permute-start | bytes 98312 | tf_op jit(solution)/shard_map/ppermute | solution.py:11
  63.5 1.0 copy-start.2
  68.9 11.0 %all-to-all-start.1 = ((f32[4,8,1024]{2,1,0:T(8,128)}), f32[4,8,1024]{2,1,0:T(8,128)S(1)}, u32[]{:S(2)}, u32[]{:S(2)}) async-start(f32[4,8,1024]{2,1,0:T(8,128)} %fusion.5), calls=%async_computation.1 | async-start | bytes 262144 | tf_op jit(solution)/shard_map/all_to_all | solution.py:94
  72.2 69.3 %reduce-scatter.6.cloned.1.call-start = ((), (), s32[]{:S(2)}) async-start(), calls=%async_computation.12 | async-start | bytes 1179648 | tf_op jit(solution)/shard_map/reduce_scatter | solution.py:126
  75.1 105.6 %reduce-scatter.4.cloned.1.call-start = ((), (), s32[]{:S(2)}) async-start(), calls=%async_computation.11 | async-start | bytes 1179648 | tf_op jit(solution)/shard_map/reduce_scatter | solution.py:125
  79.9 10.9 %all-to-all-start.3 = ((f32[4,8,1024]{2,1,0:T(8,128)}), f32[4,8,1024]{2,1,0:T(8,128)S(1)}, u32[]{:S(2)}, u32[]{:S(2)}) async-start(f32[4,8,1024]{2,1,0:T(8,128)} %fusion.4), calls=%async_computation.3 | async-start | bytes 262144 | tf_op jit(solution)/shard_map/all_to_all | solution.py:94
  90.8 9.3 %all-to-all-start.5 = ((f32[4,8,1024]{2,1,0:T(8,128)}), f32[4,8,1024]{2,1,0:T(8,128)S(1)}, u32[]{:S(2)}, u32[]{:S(2)}) async-start(f32[4,8,1024]{2,1,0:T(8,128)} %fusion.3), calls=%async_computation.5 | async-start | bytes 262144 | tf_op jit(solution)/shard_map/all_to_all | solution.py:94
  100.1 9.8 %all-to-all-start.7 = ((f32[4,8,1024]{2,1,0:T(8,128)}), f32[4,8,1024]{2,1,0:T(8,128)S(1)}, u32[]{:S(2)}, u32[]{:S(2)}) async-start(f32[4,8,1024]{2,1,0:T(8,128)} %fusion.2), calls=%async_computation.7 | async-start | bytes 262144 | tf_op jit(solution)/shard_map/all_to_all | solution.py:94
Sparse Core Ops, SparseCore 0:
  67.8 34.5 reduce-scatter.7
  105.5 35.9 reduce-scatter.5
  144.7 35.9 reduce-scatter.3
where the time goes:
time: 190 us; the launch traced here: 189 us
  waiting for transfers between devices  93.7 us (49%)
  starting transfers between devices  38.4 us (20%)
  local copies, waits for them, and re-layouts  17.9 us (9%)
  matrix products  16 us (8%)
  between operations  14.4 us (8%)
  other arithmetic  8.54 us (4%)
    reduce_scatter x1, waiting for transfers between devices, per_device(): lax.psum_scatter(acc_gate, 'dp', scatter_dimension=0, tiled=True)  37.5 us
    reduce_scatter x1, waiting for transfers between devices, per_device(): lax.psum_scatter(acc_up, 'dp', scatter_dimension=0, tiled=True)  28.7 us
    all_to_all x4, starting transfers between devices, per_device(): lax.all_to_all(sending.reshape(groups, half_caps, model_width), 'expert',...  18 us
    all_to_all x4, waiting for transfers between devices, per_device(): lax.all_to_all(partial_value.reshape(groups, capacity, model_width), 'exp...  15.6 us
    all_to_all x4, starting transfers between devices, per_device(): lax.all_to_all(partial_value.reshape(groups, capacity, model_width), 'exp...  15.5 us
    all_to_all x4, waiting for transfers between devices, per_device(): lax.all_to_all(sending.reshape(groups, half_caps, model_width), 'expert',...  11.3 us
    dot_general x12, matrix products, contract_rows(): lax.dot_general(left, right, (((0,), (0,)), ((), ())), preferred_element_...  6.96 us
    dot_general x12, matrix products, contract_cols(): lax.dot_general(left, right, (((1,), (1,)), ((), ())), preferred_element_...  5.79 us
  transfers between devices with their start and end apart: 15, of which 9 were waited for; matrix products, arithmetic and copies ran while one was open for 17% of the time, Pallas kernels for 0%

commit v1 on v0

v1 whole, which is shorter than its diff:
```python
import functools

import jax
import jax.numpy as jnp
from jax import lax
from jax.experimental import pallas as pl
from jax.experimental.pallas import tpu as pltpu
from jax.sharding import PartitionSpec as P

CAPS = 8
MESH = pl.DeviceIdType.MESH
BF16 = jnp.bfloat16
F32 = jnp.float32


def dot(left, right, lc, rc):
    return lax.dot_general(
        left, right, (((lc,), (rc,)), ((), ())), preferred_element_type=F32
    )


def kernel(
    micro,
    n_exp,
    n_dp,
    routes_ref,
    probs_ref,
    go_hbm,
    x_hbm,
    wg_hbm,
    wu_hbm,
    wd_hbm,
    gin_ref,
    gg_ref,
    gu_ref,
    gd_ref,
    go_v,
    x_v,
    wg_v,
    wu_v,
    wd_v,
    a_send,
    a_buf,
    r_send,
    r_buf,
    acc,
    p1_send,
    p1_buf,
    p2_send,
    p2_buf,
    load_sem,
    a_ssem,
    a_rsem,
    r_ssem,
    r_rsem,
    p1_ssem,
    p1_rsem,
    p2_ssem,
    p2_rsem,
):
    member = lax.axis_index("expert")
    replica = lax.axis_index("dp")
    core = lax.rem(replica, 2)
    chip = lax.div(replica, 2)
    chips = n_dp // 2
    partner = {"dp": chip * 2 + 1 - core}
    window = n_exp // 2
    tokens = go_v.shape[0]
    width = go_v.shape[1]
    tok_dev = tokens // micro
    part = micro * CAPS
    rows = n_exp * part
    row_block = width // n_dp

    def member_at(k):
        return lax.rem(member + k, n_exp)

    def chip_at(k):
        return {"dp": lax.rem(chip + k, chips) * 2 + core}

    loads = [
        pltpu.make_async_copy(src, dst, load_sem.at[i])
        for i, (src, dst) in enumerate(
            ((go_hbm, go_v), (x_hbm, x_v), (wg_hbm, wg_v), (wu_hbm, wu_v), (wd_hbm, wd_v))
        )
    ]
    for load in loads:
        load.start()

    barrier = pltpu.get_barrier_semaphore()
    for k in range(1, n_exp):
        pl.semaphore_signal(
            barrier, inc=1, device_id={"expert": member_at(k)}, device_id_type=MESH
        )
    pl.semaphore_signal(barrier, inc=1, device_id=partner, device_id_type=MESH)
    for k in range(1, chips):
        pl.semaphore_signal(barrier, inc=1, device_id=chip_at(k), device_id_type=MESH)

    column = lax.broadcasted_iota(jnp.int32, (tokens, rows), 1)
    token = lax.broadcasted_iota(jnp.int32, (tokens, rows), 0)
    expert_of = lax.div(column, 2 * part)
    ids = routes_ref[...]
    probs = probs_ref[...].astype(F32)
    hits = jnp.zeros((tokens, rows), F32)
    weights = jnp.zeros((tokens, rows), F32)
    for e in range(window):
        named = ids == e
        hit = jnp.sum(jnp.where(named, 1.0, 0.0), axis=1, keepdims=True)
        weight = jnp.sum(jnp.where(named, probs, 0.0), axis=1, keepdims=True)
        hits = jnp.where(expert_of == e, hit, hits)
        weights = jnp.where(expert_of == e, weight, weights)
    ti = lax.broadcasted_iota(jnp.int32, (tokens, tokens), 0)
    tj = lax.broadcasted_iota(jnp.int32, (tokens, tokens), 1)
    earlier = jnp.where((ti > tj) & (lax.div(ti, tok_dev) == lax.div(tj, tok_dev)), 1.0, 0.0)
    ranking = dot(earlier.astype(BF16), hits.astype(BF16), 1, 0)
    chosen = (
        (hits > 0.5)
        & (ranking == lax.rem(column, CAPS).astype(F32))
        & (lax.div(token, tok_dev) == lax.rem(lax.div(column, CAPS), micro))
    )
    mixing = jnp.where(chosen, 1.0, 0.0).astype(BF16)
    picking = jnp.where(chosen, weights, 0.0).astype(BF16)

    loads[0].wait()
    sending = dot(picking, go_v[...], 0, 0).astype(BF16)
    for h in range(n_exp):
        a_send[h] = sending[h * part : (h + 1) * part]
    pl.semaphore_wait(barrier, n_exp - 1 + chips)
    a_copies = []
    for k in range(1, n_exp):
        copy = pltpu.make_async_remote_copy(
            src_ref=a_send.at[member_at(k)],
            dst_ref=a_buf.at[member],
            send_sem=a_ssem.at[k - 1],
            recv_sem=a_rsem.at[k - 1],
            device_id={"expert": member_at(k)},
            device_id_type=MESH,
        )
        copy.start()
        a_copies.append(copy)
    a_buf[member] = a_send[member]

    loads[1].wait()
    ri = lax.broadcasted_iota(jnp.int32, (rows, rows), 0)
    rj = lax.broadcasted_iota(jnp.int32, (rows, rows), 1)
    wanted = (
        lax.rem(lax.div(ri, CAPS), micro) * (n_exp * CAPS)
        + lax.div(ri, part) * CAPS
        + lax.rem(ri, CAPS)
    )
    inputs = dot(jnp.where(rj == wanted, 1.0, 0.0).astype(BF16), x_v[...], 1, 0).astype(BF16)
    loads[2].wait()
    gate = dot(inputs, wg_v[...], 1, 0)
    loads[3].wait()
    up = dot(inputs, wu_v[...], 1, 0)
    sigmoid = jax.nn.sigmoid(gate)
    activated = gate * sigmoid
    hidden = (activated * up).astype(BF16)
    slope = up * sigmoid * (1.0 + gate * (1.0 - sigmoid))
    loads[4].wait()

    def p1_copy(o):
        return pltpu.make_async_remote_copy(
            src_ref=p1_send.at[o, 1 - core],
            dst_ref=p1_buf.at[o],
            send_sem=p1_ssem.at[o],
            recv_sem=p1_rsem.at[o],
            device_id=partner,
            device_id_type=MESH,
        )

    def store_terms(o, value):
        for d in range(n_dp):
            block = value[d * row_block : (d + 1) * row_block]
            acc[o, d % 2, d // 2] = block
            p1_send[o, d % 2, d // 2] = block.astype(BF16)

    for copy in a_copies:
        copy.wait_recv()
    scaled = a_buf[...].reshape(rows, width)
    store_terms(0, dot(scaled, hidden, 0, 0))
    p1_copies = [p1_copy(0)]
    p1_copies[0].start()

    dhidden = dot(scaled, wd_v[...], 1, 1)
    d_gate = (dhidden * slope).astype(BF16)
    d_up = (dhidden * activated).astype(BF16)
    returning = (dot(d_gate, wg_v[...], 1, 1) + dot(d_up, wu_v[...], 1, 1)).astype(BF16)
    for h in range(n_exp):
        r_send[h] = returning[h * part : (h + 1) * part]
    r_copies = []
    for k in range(1, n_exp):
        copy = pltpu.make_async_remote_copy(
            src_ref=r_send.at[member_at(k)],
            dst_ref=r_buf.at[member],
            send_sem=r_ssem.at[k - 1],
            recv_sem=r_rsem.at[k - 1],
            device_id={"expert": member_at(k)},
            device_id_type=MESH,
        )
        copy.start()
        r_copies.append(copy)
    r_buf[member] = r_send[member]

    for o, grads in ((1, d_gate), (2, d_up)):
        store_terms(o, dot(inputs, grads, 0, 0))
        p1_copies.append(p1_copy(o))
        p1_copies[o].start()

    p2_copies = []
    for o in range(3):
        p1_copies[o].wait_recv()
        for q in range(chips):
            p2_send[o, q] = (acc[o, core, q] + p1_buf[o, q].astype(F32)).astype(BF16)
        for k in range(1, chips):
            copy = pltpu.make_async_remote_copy(
                src_ref=p2_send.at[o, lax.rem(chip + k, chips)],
                dst_ref=p2_buf.at[o, k - 1],
                send_sem=p2_ssem.at[o, k - 1],
                recv_sem=p2_rsem.at[o, k - 1],
                device_id=chip_at(k),
                device_id_type=MESH,
            )
            copy.start()
            p2_copies.append(copy)

    for copy in r_copies:
        copy.wait_recv()
    gin_ref[...] = dot(mixing, r_buf[...].reshape(rows, width), 1, 0).astype(BF16)

    factor = 1.0 / (micro * n_dp)
    for o, out in enumerate((gd_ref, gg_ref, gu_ref)):
        total = acc[o, core, chip] + p1_buf[o, chip].astype(F32)
        for k in range(1, chips):
            p2_copies[o * (chips - 1) + k - 1].wait_recv()
            total = total + p2_buf[o, k - 1].astype(F32)
        out[...] = total * factor
    for copy in a_copies + r_copies + p1_copies + p2_copies:
        copy.wait_send()


def per_device(n_exp, n_dp, grad_out, routes, route_probs, dispatched, w_gate, w_up, w_down):
    micro, tok_dev, width = grad_out.shape
    cols = w_gate.shape[1]
    tokens = micro * tok_dev
    part = micro * CAPS
    rows = n_exp * part
    chips = n_dp // 2
    row_block = width // n_dp
    vmem = pl.BlockSpec(memory_space=pltpu.VMEM)
    hbm = pl.BlockSpec(memory_space=pl.ANY)
    grad = jax.ShapeDtypeStruct((row_block, cols), F32)
    dma = pltpu.SemaphoreType.DMA
    others = max(chips - 1, 1)
    out = pl.pallas_call(
        functools.partial(kernel, micro, n_exp, n_dp),
        out_shape=(jax.ShapeDtypeStruct((tokens, width), BF16), grad, grad, grad),
        in_specs=[vmem, vmem, hbm, hbm, hbm, hbm, hbm],
        out_specs=(vmem, vmem, vmem, vmem),
        scratch_shapes=[
            pltpu.VMEM((tokens, width), BF16),
            pltpu.VMEM((rows, width), BF16),
            pltpu.VMEM((width, cols), BF16),
            pltpu.VMEM((width, cols), BF16),
            pltpu.VMEM((cols, width), BF16),
            pltpu.VMEM((n_exp, part, width), BF16),
            pltpu.VMEM((n_exp, part, width), BF16),
            pltpu.VMEM((n_exp, part, width), BF16),
            pltpu.VMEM((n_exp, part, width), BF16),
            pltpu.VMEM((3, 2, chips, row_block, cols), F32),
            pltpu.VMEM((3, 2, chips, row_block, cols), BF16),
            pltpu.VMEM((3, chips, row_block, cols), BF16),
            pltpu.VMEM((3, chips, row_block, cols), BF16),
            pltpu.VMEM((3, others, row_block, cols), BF16),
            dma((5,)),
            dma((n_exp - 1,)),
            dma((n_exp - 1,)),
            dma((n_exp - 1,)),
            dma((n_exp - 1,)),
            dma((3,)),
            dma((3,)),
            dma((3, others)),
            dma((3, others)),
        ],
        compiler_params=pltpu.CompilerParams(collective_id=0, has_side_effects=True),
    )(
        routes.reshape(tokens, -1),
        route_probs.reshape(tokens, -1),
        grad_out.reshape(tokens, width),
        dispatched.reshape(rows, width),
        w_gate,
        w_up,
        w_down,
    )
    return (out[0].reshape(micro, tok_dev, width),) + tuple(out[1:])


def solution(mesh):
    return jax.shard_map(
        functools.partial(per_device, mesh.shape["expert"], mesh.shape["dp"]),
        mesh=mesh,
        in_specs=(
            P(None, ("dp", "expert"), None),
            P(None, ("dp", "expert"), None),
            P(None, ("dp", "expert"), None),
            P(None, ("dp", "expert"), None),
            P(None, "expert"),
            P(None, "expert"),
            P("expert", None),
        ),
        out_specs=(
            P(None, ("dp", "expert"), None),
            P("dp", "expert"),
            P("dp", "expert"),
            P("dp", "expert"),
        ),
        check_vma=False,
    )
```

time: 190 us -> 33.7 us (0.18)
  waiting for transfers between devices: 93.7 us -> 0 us
  starting transfers between devices: 38.4 us -> 0 us
  Pallas kernels: 0 us -> 26.1 us
  matrix products: 16 us -> 0 us
  between operations: 14.4 us -> 0.66 us
  local copies, waits for them, and re-layouts: 17.9 us -> 6.66 us
  other arithmetic: 8.54 us -> 0 us
    reduce_scatter x3 -> x0, waiting for transfers between devices: 66.2 us -> none  [the longest x1 37.5 us: per_device(): lax.psum_scatter(acc_gate, 'dp', scatter_dimension=0, tiled=True)]
    all_to_all x8 -> x0, starting transfers between devices: 33.5 us -> none  [the longest x4 18 us: per_device(): lax.all_to_all(sending.reshape(groups, half_caps, model_width), 'expert',...]
    all_to_all x8 -> x0, waiting for transfers between devices: 26.9 us -> none  [the longest x4 15.6 us: per_device(): lax.all_to_all(partial_value.reshape(groups, capacity, model_width), 'exp...]
    pallas_call x0 -> x1, Pallas kernels: none -> 26.1 us  [per_device(): pl.pallas_call(functools.partial(kernel, micro, n_exp, n_dp), out_shape=(...]
    dot_general x36 -> x0, matrix products: 16 us -> none  [the longest x12 6.96 us: contract_rows(): lax.dot_general(left, right, (((0,), (0,)), ((), ())), preferred_element_...]
    gather x16 -> x0, local copies, waits for them, and re-layouts: 5.78 us -> none  [the longest x12 3.41 us: slot_take(): weights = jnp.take_along_axis(flat_probs, position, axis=1)]
    ppermute x4 -> x0, starting transfers between devices: 4.82 us -> none  [swapped(): lax.ppermute(x, axis, [(i, i ^ 1 << stride) for i in range(lax.axis_size(...]
    another operation x9 -> x0, other arithmetic: 4.08 us -> none
  transfers between devices with their start and end apart: 15 -> 0, of which waited for: 9 -> 0; matrix products, arithmetic and copies ran while one was open for 17% -> 0% of each run, Pallas kernels for 0% -> 0%
where the time goes in v1:
time: 33.7 us; the launch traced here: 33.4 us
  Pallas kernels  26.1 us (77%)
  local copies, waits for them, and re-layouts  6.66 us (20%)
  between operations  0.66 us (2%)
    pallas_call x1, Pallas kernels, per_device(): pl.pallas_call(functools.partial(kernel, micro, n_exp, n_dp), out_shape=(...  26.1 us
    unnamed x14, local copies, waits for them, and re-layouts  6.66 us

profile of v1, /device:TPU:0, one launch (start us, length us, event | category | flops | bytes accessed | tf_op | source)
XLA Modules:
  0.0 33.4 jit_solution(8036435019816916394)
XLA Ops:
  0.6 0.0 copy-start.3
  0.6 1.4 %copy.12 = bf16[4,64,8]{2,1,0:T(8,128)(2,1)} copy(bf16[4,64,8]{1,2,0:T(8,128)(2,1)} %param.9) | data formatting | bytes 8192 | tf_op args[2]
  2.1 0.0 copy-done.3
  2.1 0.8 %copy.11 = s32[4,64,8]{2,1,0:T(8,128)} copy(s32[4,64,8]{1,2,0:T(8,128)S(1)} %copy-done.3) | data formatting | bytes 16384 | tf_op args[1]
  2.8 26.1 %shard_map.102 = (bf16[256,1024]{1,0:T(8,128)(2,1)}, f32[128,256]{1,0:T(8,128)}, f32[128,256]{1,0:T(8,128)}, f32[128,256]{1,0:T(8,128)}) custom-call(s32[256,8]{1,0:T(8,128)} %bitcast.6, bf16[256,8]{1,0:T(8,128)(2,1)} %bitcast.9, bf16[256,1024]{1,0:T(8,128)(2,1)} %bitcast.5, bf16[128,1024]{1,0:T(8,128)(2,1)} %bitcast.8, bf16[1024,256]{1,0:T(8,128)(2,1)} %wg_hbm.1, ...), custom_call_target="tpu_custom_call" | custom-call | tf_op jit(solution)/shard_map/pallas_call | solution.py:255
  28.9 0.0 copy-start.2
  28.9 1.9 %copy.17 = bf16[4,64,1024]{2,1,0:T(8,128)(2,1)} copy(bf16[4,64,1024]{2,1,0:T(8,128)(2,1)} %bitcast.7) | data formatting | bytes 1048576
  30.8 0.0 copy-done.2
  30.8 0.0 copy-start.1
  30.8 0.7 %copy.18 = f32[128,256]{1,0:T(8,128)} copy(f32[128,256]{1,0:T(8,128)S(1)} %copy-done.2) | data formatting | bytes 262144
  31.5 0.3 copy-done.1
  31.8 0.0 copy-start
  31.8 0.7 %copy.19 = f32[128,256]{1,0:T(8,128)} copy(f32[128,256]{1,0:T(8,128)S(1)} %copy-done.1) | data formatting | bytes 262144
  32.4 0.3 copy-done
  32.7 0.7 %copy.20 = f32[128,256]{1,0:T(8,128)} copy(f32[128,256]{1,0:T(8,128)S(1)} %copy-done) | data formatting | bytes 262144
Async XLA Ops:
  0.6 1.4 %copy-start.3 = (s32[4,64,8]{1,2,0:T(8,128)S(1)}, s32[4,64,8]{1,2,0:T(8,128)}, u32[]{:S(2)}) copy-start(s32[4,64,8]{1,2,0:T(8,128)} %param.8) | copy-start | bytes 24580
  28.9 1.9 %copy-start.2 = (f32[128,256]{1,0:T(8,128)S(1)}, f32[128,256]{1,0:T(8,128)}, u32[]{:S(2)}) copy-start(f32[128,256]{1,0:T(8,128)} %get-tuple-element.17) | copy-start | bytes 393220
  30.8 1.0 %copy-start.1 = (f32[128,256]{1,0:T(8,128)S(1)}, f32[128,256]{1,0:T(8,128)}, u32[]{:S(2)}) copy-start(f32[128,256]{1,0:T(8,128)} %get-tuple-element.18) | copy-start | bytes 393220
  31.8 1.0 %copy-start = (f32[128,256]{1,0:T(8,128)S(1)}, f32[128,256]{1,0:T(8,128)}, u32[]{:S(2)}) copy-start(f32[128,256]{1,0:T(8,128)} %get-tuple-element.19) | copy-start | bytes 393220

commit v2 on v1

--- a/solution.py
+++ b/solution.py
@@ -17,6 +17,15 @@
     return lax.dot_general(
         left, right, (((lc,), (rc,)), ((), ())), preferred_element_type=F32
     )
+
+
+def flipped(index, bits):
+    step = 1
+    while step <= bits:
+        if bits & step:
+            index = index + step - 2 * step * lax.rem(lax.div(index, step), 2)
+        step *= 2
+    return index
 
 
 def kernel(
@@ -73,10 +82,10 @@
     row_block = width // n_dp
 
     def member_at(k):
-        return lax.rem(member + k, n_exp)
+        return flipped(member, k)
 
     def chip_at(k):
-        return {"dp": lax.rem(chip + k, chips) * 2 + core}
+        return {"dp": flipped(chip, k) * 2 + core}
 
     loads = [
         pltpu.make_async_copy(src, dst, load_sem.at[i])
@@ -96,38 +105,41 @@
     for k in range(1, chips):
         pl.semaphore_signal(barrier, inc=1, device_id=chip_at(k), device_id_type=MESH)
 
-    column = lax.broadcasted_iota(jnp.int32, (tokens, rows), 1)
-    token = lax.broadcasted_iota(jnp.int32, (tokens, rows), 0)
-    expert_of = lax.div(column, 2 * part)
-    ids = routes_ref[...]
-    probs = probs_ref[...].astype(F32)
-    hits = jnp.zeros((tokens, rows), F32)
-    weights = jnp.zeros((tokens, rows), F32)
+    ids = jnp.concatenate([routes_ref[m] for m in range(micro)], axis=1)
+    probs = jnp.concatenate([probs_ref[m].astype(F32) for m in range(micro)], axis=1)
+    pad = max(window, 8)
+    expert_row = lax.broadcasted_iota(jnp.int32, (pad, tokens), 0)
+    hits, weights = [], []
+    table = jnp.zeros((pad, tokens), F32)
     for e in range(window):
         named = ids == e
-        hit = jnp.sum(jnp.where(named, 1.0, 0.0), axis=1, keepdims=True)
-        weight = jnp.sum(jnp.where(named, probs, 0.0), axis=1, keepdims=True)
-        hits = jnp.where(expert_of == e, hit, hits)
-        weights = jnp.where(expert_of == e, weight, weights)
+        hits.append(jnp.sum(jnp.where(named, 1.0, 0.0), axis=0, keepdims=True))
+        weights.append(jnp.sum(jnp.where(named, probs, 0.0), axis=0, keepdims=True))
+        table = jnp.where(expert_row == e, hits[e], table)
     ti = lax.broadcasted_iota(jnp.int32, (tokens, tokens), 0)
     tj = lax.broadcasted_iota(jnp.int32, (tokens, tokens), 1)
-    earlier = jnp.where((ti > tj) & (lax.div(ti, tok_dev) == lax.div(tj, tok_dev)), 1.0, 0.0)
-    ranking = dot(earlier.astype(BF16), hits.astype(BF16), 1, 0)
-    chosen = (
-        (hits > 0.5)
-        & (ranking == lax.rem(column, CAPS).astype(F32))
-        & (lax.div(token, tok_dev) == lax.rem(lax.div(column, CAPS), micro))
-    )
-    mixing = jnp.where(chosen, 1.0, 0.0).astype(BF16)
-    picking = jnp.where(chosen, weights, 0.0).astype(BF16)
+    earlier = jnp.where((ti < tj) & (lax.div(ti, tok_dev) == lax.div(tj, tok_dev)), 1.0, 0.0)
+    ranking = dot(table.astype(BF16), earlier.astype(BF16), 1, 0)
+    slot = lax.broadcasted_iota(jnp.int32, (CAPS, tokens), 0).astype(F32)
+    batch = lax.div(lax.broadcasted_iota(jnp.int32, (CAPS, tokens), 1), tok_dev)
+    ones, scales = [], []
+    for h in range(n_exp):
+        e = h // 2
+        chosen = (hits[e] > 0.5) & (ranking[e : e + 1] == slot)
+        for m in range(micro):
+            here = chosen & (batch == m)
+            ones.append(jnp.where(here, 1.0, 0.0))
+            scales.append(jnp.where(here, weights[e], 0.0))
+    mixing = jnp.concatenate(ones, axis=0).astype(BF16)
+    picking = jnp.concatenate(scales, axis=0).astype(BF16)
 
     loads[0].wait()
-    sending = dot(picking, go_v[...], 0, 0).astype(BF16)
+    sending = dot(picking, go_v[...], 1, 0).astype(BF16)
     for h in range(n_exp):
         a_send[h] = sending[h * part : (h + 1) * part]
     pl.semaphore_wait(barrier, n_exp - 1 + chips)
     a_copies = []
-    for k in range(1, n_exp):
+    for k in range(n_exp - 1, 0, -1):
         copy = pltpu.make_async_remote_copy(
             src_ref=a_send.at[member_at(k)],
             dst_ref=a_buf.at[member],
@@ -175,46 +187,20 @@
             acc[o, d % 2, d // 2] = block
             p1_send[o, d % 2, d // 2] = block.astype(BF16)
 
-    for copy in a_copies:
-        copy.wait_recv()
-    scaled = a_buf[...].reshape(rows, width)
-    store_terms(0, dot(scaled, hidden, 0, 0))
-    p1_copies = [p1_copy(0)]
-    p1_copies[0].start()
-
-    dhidden = dot(scaled, wd_v[...], 1, 1)
-    d_gate = (dhidden * slope).astype(BF16)
-    d_up = (dhidden * activated).astype(BF16)
-    returning = (dot(d_gate, wg_v[...], 1, 1) + dot(d_up, wu_v[...], 1, 1)).astype(BF16)
-    for h in range(n_exp):
-        r_send[h] = returning[h * part : (h + 1) * part]
-    r_copies = []
-    for k in range(1, n_exp):
-        copy = pltpu.make_async_remote_copy(
-            src_ref=r_send.at[member_at(k)],
-            dst_ref=r_buf.at[member],
-            send_sem=r_ssem.at[k - 1],
-            recv_sem=r_rsem.at[k - 1],
-            device_id={"expert": member_at(k)},
-            device_id_type=MESH,
-        )
-        copy.start()
-        r_copies.append(copy)
-    r_buf[member] = r_send[member]
-
-    for o, grads in ((1, d_gate), (2, d_up)):
-        store_terms(o, dot(inputs, grads, 0, 0))
+    p1_copies, p2_copies = [], []
+
+    def start_p1(o, value):
+        store_terms(o, value)
         p1_copies.append(p1_copy(o))
         p1_copies[o].start()
 
-    p2_copies = []
-    for o in range(3):
+    def start_p2(o):
         p1_copies[o].wait_recv()
-        for q in range(chips):
+        for k in range(chips - 1, 0, -1):
+            q = flipped(chip, k)
             p2_send[o, q] = (acc[o, core, q] + p1_buf[o, q].astype(F32)).astype(BF16)
-        for k in range(1, chips):
             copy = pltpu.make_async_remote_copy(
-                src_ref=p2_send.at[o, lax.rem(chip + k, chips)],
+                src_ref=p2_send.at[o, q],
                 dst_ref=p2_buf.at[o, k - 1],
                 send_sem=p2_ssem.at[o, k - 1],
                 recv_sem=p2_rsem.at[o, k - 1],
@@ -224,15 +210,44 @@
             copy.start()
             p2_copies.append(copy)
 
+    for copy in a_copies:
+        copy.wait_recv()
+    scaled = a_buf[...].reshape(rows, width)
+    start_p1(0, dot(scaled, hidden, 0, 0))
+    dhidden = dot(scaled, wd_v[...], 1, 1)
+    d_gate = (dhidden * slope).astype(BF16)
+    d_up = (dhidden * activated).astype(BF16)
+    start_p1(1, dot(inputs, d_gate, 0, 0))
+    start_p2(0)
+    returning = (dot(d_gate, wg_v[...], 1, 1) + dot(d_up, wu_v[...], 1, 1)).astype(BF16)
+    for h in range(n_exp):
+        r_send[h] = returning[h * part : (h + 1) * part]
+    r_copies = []
+    for k in range(n_exp - 1, 0, -1):
+        copy = pltpu.make_async_remote_copy(
+            src_ref=r_send.at[member_at(k)],
+            dst_ref=r_buf.at[member],
+            send_sem=r_ssem.at[k - 1],
+            recv_sem=r_rsem.at[k - 1],
+            device_id={"expert": member_at(k)},
+            device_id_type=MESH,
+        )
+        copy.start()
+        r_copies.append(copy)
+    start_p2(1)
+    start_p1(2, dot(inputs, d_up, 0, 0))
+    r_buf[member] = r_send[member]
+    start_p2(2)
+
     for copy in r_copies:
         copy.wait_recv()
-    gin_ref[...] = dot(mixing, r_buf[...].reshape(rows, width), 1, 0).astype(BF16)
+    gin_ref[...] = dot(mixing, r_buf[...].reshape(rows, width), 0, 0).astype(BF16)
 
     factor = 1.0 / (micro * n_dp)
     for o, out in enumerate((gd_ref, gg_ref, gu_ref)):
         total = acc[o, core, chip] + p1_buf[o, chip].astype(F32)
-        for k in range(1, chips):
-            p2_copies[o * (chips - 1) + k - 1].wait_recv()
+        for k in range(chips - 1, 0, -1):
+            p2_copies[o * (chips - 1) + chips - 1 - k].wait_recv()
             total = total + p2_buf[o, k - 1].astype(F32)
         out[...] = total * factor
     for copy in a_copies + r_copies + p1_copies + p2_copies:
@@ -249,12 +264,12 @@
     row_block = width // n_dp
     vmem = pl.BlockSpec(memory_space=pltpu.VMEM)
     hbm = pl.BlockSpec(memory_space=pl.ANY)
-    grad = jax.ShapeDtypeStruct((row_block, cols), F32)
+    grad = pltpu.VMEM((row_block, cols), F32)
     dma = pltpu.SemaphoreType.DMA
     others = max(chips - 1, 1)
     out = pl.pallas_call(
         functools.partial(kernel, micro, n_exp, n_dp),
-        out_shape=(jax.ShapeDtypeStruct((tokens, width), BF16), grad, grad, grad),
+        out_shape=(pltpu.VMEM((tokens, width), BF16), grad, grad, grad),
         in_specs=[vmem, vmem, hbm, hbm, hbm, hbm, hbm],
         out_specs=(vmem, vmem, vmem, vmem),
         scratch_shapes=[
@@ -284,8 +299,8 @@
         ],
         compiler_params=pltpu.CompilerParams(collective_id=0, has_side_effects=True),
     )(
-        routes.reshape(tokens, -1),
-        route_probs.reshape(tokens, -1),
+        routes.transpose(0, 2, 1),
+        route_probs.transpose(0, 2, 1),
         grad_out.reshape(tokens, width),
         dispatched.reshape(rows, width),
         w_gate,

time: 33.7 us -> 29.3 us (0.87)
  local copies, waits for them, and re-layouts: 6.66 us -> 2.76 us
  Pallas kernels: 26.1 us -> 25.6 us
    unnamed x14 -> x4, local copies, waits for them, and re-layouts: 6.66 us -> 2.76 us
    pallas_call x1, Pallas kernels: 26.1 us -> 25.6 us  [per_device(): pl.pallas_call(functools.partial(kernel, micro, n_exp, n_dp), out_shape=(...]
where the time goes in v2:
time: 29.3 us; the launch traced here: 29 us
  Pallas kernels  25.6 us (87%)
  local copies, waits for them, and re-layouts  2.76 us (9%)
  between operations  0.64 us (2%)
    pallas_call x1, Pallas kernels, per_device(): pl.pallas_call(functools.partial(kernel, micro, n_exp, n_dp), out_shape=(...  25.6 us
    unnamed x4, local copies, waits for them, and re-layouts  2.76 us

profile of v2, /device:TPU:0, one launch (start us, length us, event | category | flops | bytes accessed | tf_op | source)
XLA Modules:
  0.0 29.0 jit_solution(9244862198925410000)
XLA Ops:
  0.6 25.6 %shard_map.102 = (bf16[256,1024]{1,0:T(8,128)(2,1)S(1)}, f32[128,256]{1,0:T(8,128)S(1)}, f32[128,256]{1,0:T(8,128)S(1)}, f32[128,256]{1,0:T(8,128)S(1)}) custom-call(s32[4,8,64]{2,1,0:T(8,128)} %bitcast.8, bf16[4,8,64]{2,1,0:T(8,128)(2,1)} %bitcast.9, bf16[256,1024]{1,0:T(8,128)(2,1)} %bitcast.6, bf16[128,1024]{1,0:T(8,128)(2,1)} %bitcast.7, ...), custom_call_target="tpu_custom_call" | custom-call | tf_op jit(solution)/shard_map/pallas_call | solution.py:270
  26.2 0.8 %copy.15 = bf16[4,64,1024]{2,1,0:T(8,128)(2,1)} copy(bf16[4,64,1024]{2,1,0:T(8,128)(2,1)S(1)} %bitcast.5) | data formatting | bytes 1048576
  27.0 0.7 %copy.16 = f32[128,256]{1,0:T(8,128)} copy(f32[128,256]{1,0:T(8,128)S(1)} %get-tuple-element.13) | data formatting | bytes 262144
  27.7 0.7 %copy.17 = f32[128,256]{1,0:T(8,128)} copy(f32[128,256]{1,0:T(8,128)S(1)} %get-tuple-element.14) | data formatting | bytes 262144
  28.4 0.7 %copy.18 = f32[128,256]{1,0:T(8,128)} copy(f32[128,256]{1,0:T(8,128)S(1)} %get-tuple-element.15) | data formatting | bytes 262144

commit v3 on v2

--- a/solution.py
+++ b/solution.py
@@ -57,6 +57,8 @@
     p1_buf,
     p2_send,
     p2_buf,
+    s_all,
+    h_all,
     load_sem,
     a_ssem,
     a_rsem,
@@ -66,6 +68,10 @@
     p1_rsem,
     p2_ssem,
     p2_rsem,
+    s_ssem,
+    s_rsem,
+    h_ssem,
+    h_rsem,
 ):
     member = lax.axis_index("expert")
     replica = lax.axis_index("dp")
@@ -80,6 +86,8 @@
     part = micro * CAPS
     rows = n_exp * part
     row_block = width // n_dp
+    gather = row_block % 128 == 0
+    inner = lax.rem(lax.div(lax.rem(member, 4) + 1, 2), 2) == 1
 
     def member_at(k):
         return flipped(member, k)
@@ -101,9 +109,10 @@
         pl.semaphore_signal(
             barrier, inc=1, device_id={"expert": member_at(k)}, device_id_type=MESH
         )
-    pl.semaphore_signal(barrier, inc=1, device_id=partner, device_id_type=MESH)
-    for k in range(1, chips):
-        pl.semaphore_signal(barrier, inc=1, device_id=chip_at(k), device_id_type=MESH)
+    for k in range(1, n_dp):
+        pl.semaphore_signal(
+            barrier, inc=1, device_id={"dp": flipped(replica, k)}, device_id_type=MESH
+        )
 
     ids = jnp.concatenate([routes_ref[m] for m in range(micro)], axis=1)
     probs = jnp.concatenate([probs_ref[m].astype(F32) for m in range(micro)], axis=1)
@@ -137,19 +146,24 @@
     sending = dot(picking, go_v[...], 1, 0).astype(BF16)
     for h in range(n_exp):
         a_send[h] = sending[h * part : (h + 1) * part]
-    pl.semaphore_wait(barrier, n_exp - 1 + chips)
-    a_copies = []
-    for k in range(n_exp - 1, 0, -1):
-        copy = pltpu.make_async_remote_copy(
-            src_ref=a_send.at[member_at(k)],
-            dst_ref=a_buf.at[member],
+    pl.semaphore_wait(barrier, n_exp - 1 + n_dp - 1)
+    def a_copy(k, src, slot, to):
+        return pltpu.make_async_remote_copy(
+            src_ref=src,
+            dst_ref=a_buf.at[slot],
             send_sem=a_ssem.at[k - 1],
             recv_sem=a_rsem.at[k - 1],
-            device_id={"expert": member_at(k)},
+            device_id={"expert": to},
             device_id_type=MESH,
         )
-        copy.start()
-        a_copies.append(copy)
+
+    a_copies = {}
+    for k in range(n_exp - 1, 0, -1):
+        a_copies[k] = a_copy(k, a_send.at[member_at(k)], member, member_at(k))
+        if k == 2:
+            pl.when(jnp.logical_not(inner))(a_copies[k].start)
+        else:
+            a_copies[k].start()
     a_buf[member] = a_send[member]
 
     loads[1].wait()
@@ -161,6 +175,11 @@
         + lax.rem(ri, CAPS)
     )
     inputs = dot(jnp.where(rj == wanted, 1.0, 0.0).astype(BF16), x_v[...], 1, 0).astype(BF16)
+    if n_exp > 2:
+        across = member_at(3)
+        a_copies[3].wait_recv()
+        passed = a_copy(2, a_buf.at[across], across, member_at(1))
+        pl.when(inner)(passed.start)
     loads[2].wait()
     gate = dot(inputs, wg_v[...], 1, 0)
     loads[3].wait()
@@ -168,6 +187,20 @@
     sigmoid = jax.nn.sigmoid(gate)
     activated = gate * sigmoid
     hidden = (activated * up).astype(BF16)
+    h_copies, s_copies = [], []
+    if gather:
+        h_all[replica] = hidden
+        for k in range(n_dp - 1, 0, -1):
+            copy = pltpu.make_async_remote_copy(
+                src_ref=h_all.at[replica],
+                dst_ref=h_all.at[replica],
+                send_sem=h_ssem.at[k - 1],
+                recv_sem=h_rsem.at[k - 1],
+                device_id={"dp": flipped(replica, k)},
+                device_id_type=MESH,
+            )
+            copy.start()
+            h_copies.append(copy)
     slope = up * sigmoid * (1.0 + gate * (1.0 - sigmoid))
     loads[4].wait()
 
@@ -187,11 +220,11 @@
             acc[o, d % 2, d // 2] = block
             p1_send[o, d % 2, d // 2] = block.astype(BF16)
 
-    p1_copies, p2_copies = [], []
+    p1_copies, p2_copies = {}, {}
 
     def start_p1(o, value):
         store_terms(o, value)
-        p1_copies.append(p1_copy(o))
+        p1_copies[o] = p1_copy(o)
         p1_copies[o].start()
 
     def start_p2(o):
@@ -208,17 +241,31 @@
                 device_id_type=MESH,
             )
             copy.start()
-            p2_copies.append(copy)
-
-    for copy in a_copies:
-        copy.wait_recv()
+            p2_copies[o, k] = copy
+
+    for k in range(1, n_exp):
+        if k != 3:
+            a_copies[k].wait_recv()
     scaled = a_buf[...].reshape(rows, width)
-    start_p1(0, dot(scaled, hidden, 0, 0))
+    if gather:
+        for k in range(n_dp - 1, 0, -1):
+            peer = flipped(replica, k)
+            columns = pl.ds(pl.multiple_of(peer * row_block, row_block), row_block)
+            copy = pltpu.make_async_remote_copy(
+                src_ref=a_buf.at[:, :, columns],
+                dst_ref=s_all.at[replica],
+                send_sem=s_ssem.at[k - 1],
+                recv_sem=s_rsem.at[k - 1],
+                device_id={"dp": peer},
+                device_id_type=MESH,
+            )
+            copy.start()
+            s_copies.append(copy)
+    else:
+        start_p1(0, dot(scaled, hidden, 0, 0))
     dhidden = dot(scaled, wd_v[...], 1, 1)
     d_gate = (dhidden * slope).astype(BF16)
     d_up = (dhidden * activated).astype(BF16)
-    start_p1(1, dot(inputs, d_gate, 0, 0))
-    start_p2(0)
     returning = (dot(d_gate, wg_v[...], 1, 1) + dot(d_up, wu_v[...], 1, 1)).astype(BF16)
     for h in range(n_exp):
         r_send[h] = returning[h * part : (h + 1) * part]
@@ -234,24 +281,63 @@
         )
         copy.start()
         r_copies.append(copy)
+    start_p1(1, dot(inputs, d_gate, 0, 0))
+    start_p1(2, dot(inputs, d_up, 0, 0))
+    if not gather:
+        start_p2(0)
+    r_buf[member] = r_send[member]
     start_p2(1)
-    start_p1(2, dot(inputs, d_up, 0, 0))
-    r_buf[member] = r_send[member]
     start_p2(2)
 
+    if gather:
+        own = pl.ds(pl.multiple_of(replica * row_block, row_block), row_block)
+        s_all[replica] = a_buf[:, :, own]
+        for copy in h_copies + s_copies:
+            copy.wait_recv()
+        slots = n_dp * rows
+        down = dot(
+            s_all[...].reshape(slots, row_block), h_all[...].reshape(slots, wg_v.shape[1]), 0, 0
+        )
+        gd_ref[...] = down * (1.0 / (micro * n_dp))
     for copy in r_copies:
         copy.wait_recv()
     gin_ref[...] = dot(mixing, r_buf[...].reshape(rows, width), 0, 0).astype(BF16)
 
     factor = 1.0 / (micro * n_dp)
     for o, out in enumerate((gd_ref, gg_ref, gu_ref)):
+        if o not in p1_copies:
+            continue
         total = acc[o, core, chip] + p1_buf[o, chip].astype(F32)
         for k in range(chips - 1, 0, -1):
-            p2_copies[o * (chips - 1) + chips - 1 - k].wait_recv()
+            p2_copies[o, k].wait_recv()
             total = total + p2_buf[o, k - 1].astype(F32)
         out[...] = total * factor
-    for copy in a_copies + r_copies + p1_copies + p2_copies:
+    started = [*a_copies.values(), *p1_copies.values(), *p2_copies.values()]
+    for copy in started + r_copies + h_copies + s_copies:
         copy.wait_send()
+
+
+def settle(*refs):
+    count = len(refs) // 2
+    sem = refs[-1]
+    copies = [
+        pltpu.make_async_copy(refs[i], refs[count + i], sem.at[i]) for i in range(count)
+    ]
+    for copy in copies:
+        copy.start()
+    for copy in copies:
+        copy.wait()
+
+
+def settled(arrays):
+    anywhere = pl.BlockSpec(memory_space=pl.ANY)
+    return pl.pallas_call(
+        settle,
+        out_shape=tuple(jax.ShapeDtypeStruct(a.shape, a.dtype) for a in arrays),
+        in_specs=[pl.BlockSpec(memory_space=pltpu.VMEM)] * len(arrays),
+        out_specs=(anywhere,) * len(arrays),
+        scratch_shapes=[pltpu.SemaphoreType.DMA((len(arrays),))],
+    )(*[pltpu.with_memory_space_constraint(a, pltpu.VMEM) for a in arrays])
 
 
 def per_device(n_exp, n_dp, grad_out, routes, route_probs, dispatched, w_gate, w_up, w_down):
@@ -267,6 +353,7 @@
     grad = pltpu.VMEM((row_block, cols), F32)
     dma = pltpu.SemaphoreType.DMA
     others = max(chips - 1, 1)
+    gather = row_block % 128 == 0
     out = pl.pallas_call(
         functools.partial(kernel, micro, n_exp, n_dp),
         out_shape=(pltpu.VMEM((tokens, width), BF16), grad, grad, grad),
@@ -287,6 +374,8 @@
             pltpu.VMEM((3, chips, row_block, cols), BF16),
             pltpu.VMEM((3, chips, row_block, cols), BF16),
             pltpu.VMEM((3, others, row_block, cols), BF16),
+            pltpu.VMEM((n_dp, n_exp, part, row_block) if gather else (8, 128), BF16),
+            pltpu.VMEM((n_dp, rows, cols) if gather else (8, 128), BF16),
             dma((5,)),
             dma((n_exp - 1,)),
             dma((n_exp - 1,)),
@@ -296,6 +385,10 @@
             dma((3,)),
             dma((3, others)),
             dma((3, others)),
+            dma((n_dp - 1,)),
+            dma((n_dp - 1,)),
+            dma((n_dp - 1,)),
+            dma((n_dp - 1,)),
         ],
         compiler_params=pltpu.CompilerParams(collective_id=0, has_side_effects=True),
     )(
@@ -307,6 +400,7 @@
         w_up,
         w_down,
     )
+    out = settled(out)
     return (out[0].reshape(micro, tok_dev, width),) + tuple(out[1:])
 
 

time: 29.3 us -> 28.9 us (0.986)
  local copies, waits for them, and re-layouts: 2.76 us -> 0 us
  Pallas kernels: 25.6 us -> 27.9 us
    unnamed x4 -> x0, local copies, waits for them, and re-layouts: 2.76 us -> none
    pallas_call x1, Pallas kernels: 25.6 us -> 27 us  [per_device(): pl.pallas_call(functools.partial(kernel, micro, n_exp, n_dp), out_shape=(...]
    pallas_call x0 -> x1, Pallas kernels: none -> 0.95 us  [settled(): pl.pallas_call(settle, out_shape=tuple((jax.ShapeDtypeStruct(a.shape, a.d...]
where the time goes in v3:
time: 28.9 us; the launch traced here: 28.6 us
  Pallas kernels  27.9 us (97%)
  between operations  0.64 us (2%)
    pallas_call x1, Pallas kernels, per_device(): pl.pallas_call(functools.partial(kernel, micro, n_exp, n_dp), out_shape=(...  27 us
    pallas_call x1, Pallas kernels, settled(): pl.pallas_call(settle, out_shape=tuple((jax.ShapeDtypeStruct(a.shape, a.d...  0.95 us

profile of v3, /device:TPU:0, one launch (start us, length us, event | category | flops | bytes accessed | tf_op | source)
XLA Modules:
  0.0 28.6 jit_solution(1974848790035823244)
XLA Ops:
  0.6 27.0 %shard_map.102 = (bf16[256,1024]{1,0:T(8,128)(2,1)S(1)}, f32[128,256]{1,0:T(8,128)S(1)}, f32[128,256]{1,0:T(8,128)S(1)}, f32[128,256]{1,0:T(8,128)S(1)}) custom-call(s32[4,8,64]{2,1,0:T(8,128)} %bitcast.7, bf16[4,8,64]{2,1,0:T(8,128)(2,1)} %bitcast.8, bf16[256,1024]{1,0:T(8,128)(2,1)} %bitcast.5, bf16[128,1024]{1,0:T(8,128)(2,1)} %bitcast.6, ...), custom_call_target="tpu_custom_call" | custom-call | tf_op jit(solution)/shard_map/pallas_call | solution.py:357
  27.6 1.0 %shard_map.103 = (bf16[256,1024]{1,0:T(8,128)(2,1)}, f32[128,256]{1,0:T(8,128)}, f32[128,256]{1,0:T(8,128)}, f32[128,256]{1,0:T(8,128)}) custom-call(bf16[256,1024]{1,0:T(8,128)(2,1)S(1)} %get-tuple-element.12.refs_0_, f32[128,256]{1,0:T(8,128)S(1)} %get-tuple-element.13.refs_1_, f32[128,256]{1,0:T(8,128)S(1)} %get-tuple-element.14.refs_2_, ...), custom_call_target="tpu_custom_call" | custom-call | tf_op jit(solution)/shard_map/pallas_call | solution.py:334

commit v4 on v3

--- a/solution.py
+++ b/solution.py
@@ -87,7 +87,6 @@
     rows = n_exp * part
     row_block = width // n_dp
     gather = row_block % 128 == 0
-    inner = lax.rem(lax.div(lax.rem(member, 4) + 1, 2), 2) == 1
 
     def member_at(k):
         return flipped(member, k)
@@ -158,12 +157,9 @@
         )
 
     a_copies = {}
-    for k in range(n_exp - 1, 0, -1):
+    for k in range(1, n_exp):
         a_copies[k] = a_copy(k, a_send.at[member_at(k)], member, member_at(k))
-        if k == 2:
-            pl.when(jnp.logical_not(inner))(a_copies[k].start)
-        else:
-            a_copies[k].start()
+        a_copies[k].start()
     a_buf[member] = a_send[member]
 
     loads[1].wait()
@@ -175,11 +171,6 @@
         + lax.rem(ri, CAPS)
     )
     inputs = dot(jnp.where(rj == wanted, 1.0, 0.0).astype(BF16), x_v[...], 1, 0).astype(BF16)
-    if n_exp > 2:
-        across = member_at(3)
-        a_copies[3].wait_recv()
-        passed = a_copy(2, a_buf.at[across], across, member_at(1))
-        pl.when(inner)(passed.start)
     loads[2].wait()
     gate = dot(inputs, wg_v[...], 1, 0)
     loads[3].wait()
@@ -244,8 +235,7 @@
             p2_copies[o, k] = copy
 
     for k in range(1, n_exp):
-        if k != 3:
-            a_copies[k].wait_recv()
+        a_copies[k].wait_recv()
     scaled = a_buf[...].reshape(rows, width)
     if gather:
         for k in range(n_dp - 1, 0, -1):

time: 28.9 us -> 25.3 us (0.88)
  Pallas kernels: 27.9 us -> 24.3 us
    pallas_call x1, Pallas kernels: 27 us -> 23.4 us  [per_device(): pl.pallas_call(functools.partial(kernel, micro, n_exp, n_dp), out_shape=(...]
where the time goes in v4:
time: 25.3 us; the launch traced here: 25 us
  Pallas kernels  24.3 us (96%)
  between operations  0.64 us (3%)
    pallas_call x1, Pallas kernels, per_device(): pl.pallas_call(functools.partial(kernel, micro, n_exp, n_dp), out_shape=(...  23.4 us
    pallas_call x1, Pallas kernels, settled(): pl.pallas_call(settle, out_shape=tuple((jax.ShapeDtypeStruct(a.shape, a.d...  0.95 us

profile of v4, /device:TPU:0, one launch (start us, length us, event | category | flops | bytes accessed | tf_op | source)
XLA Modules:
  0.0 25.0 jit_solution(17597871030325692086)
XLA Ops:
  0.6 23.4 %shard_map.102 = (bf16[256,1024]{1,0:T(8,128)(2,1)S(1)}, f32[128,256]{1,0:T(8,128)S(1)}, f32[128,256]{1,0:T(8,128)S(1)}, f32[128,256]{1,0:T(8,128)S(1)}) custom-call(s32[4,8,64]{2,1,0:T(8,128)} %bitcast.7, bf16[4,8,64]{2,1,0:T(8,128)(2,1)} %bitcast.8, bf16[256,1024]{1,0:T(8,128)(2,1)} %bitcast.5, bf16[128,1024]{1,0:T(8,128)(2,1)} %bitcast.6, ...), custom_call_target="tpu_custom_call" | custom-call | tf_op jit(solution)/shard_map/pallas_call | solution.py:347
  24.0 1.0 %shard_map.103 = (bf16[256,1024]{1,0:T(8,128)(2,1)}, f32[128,256]{1,0:T(8,128)}, f32[128,256]{1,0:T(8,128)}, f32[128,256]{1,0:T(8,128)}) custom-call(bf16[256,1024]{1,0:T(8,128)(2,1)S(1)} %get-tuple-element.12.refs_0_, f32[128,256]{1,0:T(8,128)S(1)} %get-tuple-element.13.refs_1_, f32[128,256]{1,0:T(8,128)S(1)} %get-tuple-element.14.refs_2_, ...), custom_call_target="tpu_custom_call" | custom-call | tf_op jit(solution)/shard_map/pallas_call | solution.py:324
